TPU v7x, 256 devices: a whole 4x4x8 slice. The times are simulated.
256 devices in a mesh: snap: 8 (over z), vert: 32 (over x, y, core).
Axes of the slice: x: 4, y: 4, z: 8, core: 2. Of those that a mesh axis runs over, the one named last changes fastest.
Arguments:
- features: bfloat16 [16, 65536, 256], P('snap', 'vert'), may hold values from -6 to 6
- tile_rows: int32 [16, 2048], P('snap', 'vert'), may hold values from 0 to 15
- tile_cols: int32 [16, 2048], P('snap', 'vert'), may hold values from 0 to 21
- tile_vals: bfloat16 [16, 2048, 128, 128], P('snap', 'vert'), may hold values from -0.25 to 0.25
- send_lists: int32 [32, 6], replicated, may hold values from 0 to 15
- conv1_weight: bfloat16 [256, 256], replicated, may hold values from -0.375 to 0.375
- conv2_weight: bfloat16 [256, 256], replicated, may hold values from -0.375 to 0.375
- lstm_weight: bfloat16 [2, 512, 1024], replicated, may hold values from -0.25 to 0.25
- lstm_bias: float32 [2, 1024], replicated, may hold values from -4 to 4
Outputs:
- mixed: bfloat16 [16, 65536, 256], P('snap', 'vert')
All inputs are finite; a program needn't handle non-finite values.
Results may differ from a plain program's by a relative error of at most 0.007.
Values may be sent and summed in bfloat16 or wider, within the bound.
A program may use at most 128 MiB of HBM per device.

v0:
```python
import jax
import jax.numpy as jnp
from jax import lax
from jax.sharding import PartitionSpec as P

BS = 128


def with_halo(block, sides, width):
    for axis, dim in sides:
        count = lax.axis_size(axis)
        forward = [(i, i + 1) for i in range(count - 1)]
        forward.append((count - 1, 0))
        backward = [(target, source) for source, target in forward]
        low = lax.ppermute(
            lax.slice_in_dim(block, block.shape[dim] - width, None, axis=dim), axis, forward
        )
        high = lax.ppermute(lax.slice_in_dim(block, 0, width, axis=dim), axis, backward)
        block = jnp.concatenate([low, block, high], axis=dim)
    return block


def rims(packed, width):
    return with_halo(packed, (("vert", 1),), width)


def extend(field, send_lists, tile_cols):
    snapshots, vertices, width = field.shape
    blocks = vertices // BS
    bound = send_lists.shape[1] // 2
    device = lax.axis_index("vert")
    own_list = lax.dynamic_index_in_dim(send_lists, device, 0, keepdims=False)
    packed = jnp.take(field.reshape(snapshots, blocks, BS, width), own_list, axis=1).reshape(
        snapshots, 2 * bound * BS, width
    )
    bordered = rims(packed, bound * BS)
    extended = jnp.concatenate(
        [bordered[:, : bound * BS], field, bordered[:, bordered.shape[1] - bound * BS :]], axis=1
    )
    return (extended.reshape(snapshots, -1, BS, width), tile_cols)


def convolve(field, tile_rows, tile_cols, tile_vals, send_lists):
    snapshots, vertices, width = field.shape
    blocks = vertices // BS
    extended, position = extend(field, send_lists, tile_cols)
    picked = jax.vmap(lambda slab, where_at: jnp.take(slab, where_at, axis=0))(extended, position)
    product = jnp.einsum("skij,skjf->skif", tile_vals, picked, preferred_element_type=jnp.float32)
    onehot = (tile_rows[..., None] == jnp.arange(blocks, dtype=jnp.int32)).astype(jnp.float32)
    summed = jnp.einsum("skb,skif->sbif", onehot, product, preferred_element_type=jnp.float32)
    return summed.reshape(snapshots, vertices, width)


def project(field, weight):
    snapshots, vertices, width = field.shape
    result = jnp.dot(
        field.reshape(snapshots * vertices, width), weight, preferred_element_type=jnp.float32
    )
    return result.astype(jnp.bfloat16).reshape(snapshots, vertices, width)


def cell_step(inputs, hidden, memory, weight, bias):
    gates = (
        jnp.dot(
            jnp.concatenate([inputs, hidden], axis=-1), weight, preferred_element_type=jnp.float32
        )
        + bias
    )
    in_gate, forget, candidate, out_gate = jnp.split(gates, 4, axis=-1)
    memory = jax.nn.sigmoid(forget) * memory + jax.nn.sigmoid(in_gate) * jnp.tanh(candidate)
    hidden = (jax.nn.sigmoid(out_gate) * jnp.tanh(memory)).astype(jnp.bfloat16)
    return (hidden, memory)


def shards(
    features,
    tile_rows,
    tile_cols,
    tile_vals,
    send_lists,
    conv1_weight,
    conv2_weight,
    lstm_weight,
    lstm_bias,
):
    snapshots, vertices, width = features.shape
    projected = project(features, conv1_weight)
    convolved = jnp.maximum(
        convolve(projected, tile_rows, tile_cols, tile_vals, send_lists), 0.0
    ).astype(jnp.bfloat16)
    groups = lax.axis_size("snap")
    grouped = convolved.reshape(snapshots, groups, vertices // groups, width)
    sequence = lax.all_to_all(grouped, "snap", split_axis=1, concat_axis=0, tiled=True)[:, 0]
    count = sequence.shape[1]
    zero_h = jnp.zeros((count, width), jnp.bfloat16)
    zero_c = jnp.zeros((count, width), jnp.float32)

    def advance(carry, inputs):
        first_h, first_c, second_h, second_c = carry
        first_h, first_c = cell_step(inputs, first_h, first_c, lstm_weight[0], lstm_bias[0])
        second_h, second_c = cell_step(first_h, second_h, second_c, lstm_weight[1], lstm_bias[1])
        return ((first_h, first_c, second_h, second_c), second_h)

    carry, outputs = lax.scan(advance, (zero_h, zero_c, zero_h, zero_c), sequence)
    recurrent = outputs[:, None]
    restored = lax.all_to_all(recurrent, "snap", split_axis=0, concat_axis=1, tiled=True).reshape(
        snapshots, vertices, width
    )
    second = project(restored, conv2_weight)
    return convolve(second, tile_rows, tile_cols, tile_vals, send_lists).astype(jnp.bfloat16)


def solution(mesh):
    placed = (
        P("snap", "vert", None),
        P("snap", "vert"),
        P("snap", "vert"),
        P("snap", "vert", None, None),
        P(),
        P(),
        P(),
        P(),
        P(),
    )
    return jax.shard_map(
        shards, mesh=mesh, in_specs=placed, out_specs=P("snap", "vert", None), check_vma=False
    )
```

profile of v0, /device:TPU:31, one launch (start us, length us, event | category | flops | bytes accessed | tf_op | source)
XLA Modules:
  0.0 305.9 jit_solution(4708403883143465019)
XLA Ops:
  0.0 1.0 dynamic-slice_reduce_fusion
  1.6 2.9 convolution_convert_fusion.1
  4.5 2.2 gather_fusion
  7.0 2.2 collective-permute-start
  9.3 4.6 %collective-permute-done = bf16[2,384,256]{2,1,0:T(8,128)(2,1)S(1)} collective-permute-done((bf16[2,384,256]{2,1,0:T(8,128)(2,1)S(1)}, bf16[2,384,256]{2,1,0:T(8,128)(2,1)S(1)}, u32[]{:S(2)}, u32[]{:S(2)}) %collective-permute-start) | collective-permute-done | bytes 393248 | tf_op jit(solution)/shard_map/ppermute | solution.py:15
  13.9 5.8 %collective-permute-done.1 = bf16[2,384,256]{2,1,0:T(8,128)(2,1)S(1)} collective-permute-done((bf16[2,384,256]{2,1,0:T(8,128)(2,1)S(1)}, bf16[2,384,256]{2,1,0:T(8,128)(2,1)S(1)}, u32[]{:S(2)}, u32[]{:S(2)}) %collective-permute-start.1) | collective-permute-done | bytes 393248 | tf_op jit(solution)/shard_map/ppermute | solution.py:18
  20.5 1.9 pad_maximum_fusion
  22.4 7.2 %gather_fusion.1 = bf16[128,128,256]{2,1,0:T(8,128)(2,1)} fusion(bf16[2,22,128,256]{3,2,1,0:T(8,128)(2,1)S(1)} %bitcast.76, s32[128]{0:T(128)S(1)} %reshape.92), kind=kCustom, calls=%fused_computation.1.clone | custom fusion | bytes 16778240 | tf_op jit(solution)/shard_map/vmap(jit(_take))/gather | solution.py:47
  29.6 12.0 %copy.35 = bf16[2,64,128,256]{2,3,1,0:T(8,128)(2,1)} copy(bf16[2,64,128,256]{3,2,1,0:T(8,128)(2,1)} %bitcast.78) | data formatting | bytes 16777216 | tf_op jit(solution)/shard_map/vmap(jit(_take))/gather | solution.py:47
  41.6 11.6 %fusion.46 = bf16[2,64,128,256]{2,3,1,0:T(8,128)(2,1)} fusion(bf16[2,64,128,128]{3,2,1,0:T(8,128)(2,1)} %param.18, bf16[2,64,128,256]{2,3,1,0:T(8,128)(2,1)} %copy.35, pred[2,64]{1,0:T(4,128)(4,1)S(1)} %compare_and_fusion), kind=kOutput, calls=%fused_computation.64 | convolution fusion | flops 1077936128 | bytes 20971648 | tf_op jit(solution)/shard_map/skij,skjf->skif/dot_general | solution.py:48
  53.2 12.3 %copy.36 = bf16[2,64,128,256]{3,1,2,0:T(8,128)(2,1)} copy(bf16[2,64,128,256]{2,3,1,0:T(8,128)(2,1)} %fusion.46) | data formatting | bytes 16777216 | tf_op jit(solution)/shard_map/skij,skjf->skif/dot_general | solution.py:48
  65.5 4.6 %maximum_convert_fusion = bf16[2,16,128,256]{3,1,2,0:T(8,128)(2,1)S(1)} fusion(bf16[2,64,128,256]{3,1,2,0:T(8,128)(2,1)} %copy.36, s32[2,64]{1,0:T(2,128)S(1)} %copy-done.6), kind=kOutput, calls=%fused_computation.70 | convolution fusion | flops 137365504 | bytes 10486272 | tf_op jit(solution)/shard_map/skb,skif->sbif/dot_general | solution.py:50
  70.9 1.5 copy.38
  72.4 6.5 %all-to-all-start = ((bf16[2,8,256,256]{3,2,0,1:T(8,128)(2,1)}), bf16[2,8,256,256]{3,2,0,1:T(8,128)(2,1)S(1)}, u32[]{:S(2)}, u32[]{:S(2)}) async-start(bf16[2,8,256,256]{3,2,0,1:T(8,128)(2,1)} %copy.38), calls=%async_computation | async-start | bytes 4194304 | tf_op jit(solution)/shard_map/all_to_all | solution.py:93
  78.9 49.3 %all-to-all-done = bf16[2,8,256,256]{3,2,0,1:T(8,128)(2,1)S(1)} async-done(((bf16[2,8,256,256]{3,2,0,1:T(8,128)(2,1)}), bf16[2,8,256,256]{3,2,0,1:T(8,128)(2,1)S(1)}, u32[]{:S(2)}, u32[]{:S(2)}) %all-to-all-start) | async-done | bytes 2097184 | tf_op jit(solution)/shard_map/all_to_all | solution.py:93
  128.2 57.3 %while.19 = (s32[]{:T(128)}, bf16[256,256]{1,0:T(8,128)(2,1)S(1)}, f32[256,256]{1,0:T(8,128)S(1)}, bf16[256,256]{1,0:T(8,128)(2,1)S(1)}, f32[256,256]{1,0:T(8,12...) while((s32[]{:T(128)}, bf16[256,256]{1,0:T(8,128)(2,1)S(1)}, ...), condition=%wide.region_1.4_spmd.clone, body=%wide.region_0.0_spmd.clone.sunk | while | flops 540540928 | bytes 17457816 | solution.py:104
  128.3 1.8 convolution_add_fusion.4
  131.9 1.8 convolution_add_fusion.4
  134.4 0.9 bitcast_dynamic-update-slice_fusion.2
  135.5 1.8 convolution_add_fusion.4
  138.0 0.9 bitcast_dynamic-update-slice_fusion.2
  139.0 1.8 convolution_add_fusion.4
  141.6 0.9 bitcast_dynamic-update-slice_fusion.2
  142.6 1.8 convolution_add_fusion.4
  145.2 0.9 bitcast_dynamic-update-slice_fusion.2
  146.2 1.8 convolution_add_fusion.4
  148.8 0.9 bitcast_dynamic-update-slice_fusion.2
  149.8 1.8 convolution_add_fusion.4
  153.4 1.8 convolution_add_fusion.4
  157.0 1.8 convolution_add_fusion.4
  160.5 1.8 convolution_add_fusion.4
  164.1 1.8 convolution_add_fusion.4
  167.7 1.8 convolution_add_fusion.4
  171.3 1.8 convolution_add_fusion.4
  174.9 1.8 convolution_add_fusion.4
  178.5 1.8 convolution_add_fusion.4
  182.0 1.8 convolution_add_fusion.4
  185.6 54.9 %all_to_all.30 = bf16[16,1,256,256]{3,2,1,0:T(8,128)(2,1)S(1)} all-to-all(bf16[16,1,256,256]{3,2,1,0:T(8,128)(2,1)} %bitcast.89), channel_id=1, replica_groups=mesh['snap'=8,'vert'=32] {'snap'}, dimensions={0} | all-to-all | bytes 4194304 | tf_op jit(solution)/shard_map/all_to_all | solution.py:106
  242.3 1.4 collective-permute-start.2
  243.7 4.7 %collective-permute-done.2 = bf16[2,384,256]{2,1,0:T(8,128)(2,1)S(1)} collective-permute-done((bf16[2,384,256]{2,1,0:T(8,128)(2,1)S(1)}, bf16[2,384,256]{2,1,0:T(8,128)(2,1)S(1)}, u32[]{:S(2)}, u32[]{:S(2)}) %collective-permute-start.2) | collective-permute-done | bytes 393248 | tf_op jit(solution)/shard_map/ppermute | solution.py:15
  248.4 5.8 %collective-permute-done.3 = bf16[2,384,256]{2,1,0:T(8,128)(2,1)S(1)} collective-permute-done((bf16[2,384,256]{2,1,0:T(8,128)(2,1)S(1)}, bf16[2,384,256]{2,1,0:T(8,128)(2,1)S(1)}, u32[]{:S(2)}, u32[]{:S(2)}) %collective-permute-start.3) | collective-permute-done | bytes 393248 | tf_op jit(solution)/shard_map/ppermute | solution.py:18
  254.2 1.8 pad_maximum_fusion.1
  256.0 7.2 %gather_fusion.3 = bf16[128,128,256]{2,1,0:T(8,128)(2,1)} fusion(bf16[2,22,128,256]{3,2,1,0:T(8,128)(2,1)S(1)} %bitcast.75, s32[128]{0:T(128)S(1)} %reshape.92), kind=kCustom, calls=%fused_computation.3.clone | custom fusion | bytes 16778240 | tf_op jit(solution)/shard_map/vmap(jit(_take))/gather | solution.py:47
  263.2 12.0 %copy.41 = bf16[2,64,128,256]{2,3,1,0:T(8,128)(2,1)} copy(bf16[2,64,128,256]{3,2,1,0:T(8,128)(2,1)} %bitcast.77) | data formatting | bytes 16777216 | tf_op jit(solution)/shard_map/vmap(jit(_take))/gather | solution.py:47
  275.2 11.6 %fusion.49 = bf16[2,64,128,256]{2,3,1,0:T(8,128)(2,1)} fusion(bf16[2,64,128,128]{3,2,1,0:T(8,128)(2,1)} %param.18, bf16[2,64,128,256]{2,3,1,0:T(8,128)(2,1)} %copy.41, pred[2,64]{1,0:T(4,128)(4,1)S(1)} %compare_and_fusion), kind=kOutput, calls=%fused_computation.65 | convolution fusion | flops 1077936128 | bytes 20971648 | tf_op jit(solution)/shard_map/skij,skjf->skif/dot_general | solution.py:48
  286.8 12.3 %copy.42 = bf16[2,64,128,256]{3,1,2,0:T(8,128)(2,1)} copy(bf16[2,64,128,256]{2,3,1,0:T(8,128)(2,1)} %fusion.49) | data formatting | bytes 16777216 | tf_op jit(solution)/shard_map/skij,skjf->skif/dot_general | solution.py:48
  299.1 4.7 %convolution_convert_fusion.2 = bf16[2,16,128,256]{3,1,2,0:T(8,128)(2,1)S(1)} fusion(bf16[2,64,128,256]{3,1,2,0:T(8,128)(2,1)} %copy.42, s32[2,64]{1,0:T(2,128)S(1)} %copy-done.6), kind=kOutput, calls=%fused_computation.73 | convolution fusion | flops 134219776 | bytes 10486272 | tf_op jit(solution)/shard_map/skb,skif->sbif/dot_general | solution.py:50
  303.8 2.1 copy.43
  (162 shorter events, 27.1 us)
Async XLA Ops:
  0.0 1.6 copy-start
  4.5 4.7 %copy-start.7 = (s32[2,64]{1,0:T(2,128)S(1)}, s32[2,64]{1,0:T(2,128)}, u32[]{:S(2)}) copy-start(s32[2,64]{1,0:T(2,128)} %param.17) | copy-start | bytes 1540
  7.0 6.9 %collective-permute-start = (bf16[2,384,256]{2,1,0:T(8,128)(2,1)S(1)}, bf16[2,384,256]{2,1,0:T(8,128)(2,1)S(1)}, u32[]{:S(2)}, u32[]{:S(2)}) collective-permute-start(bf16[2,384,256]{2,1,0:T(8,128)(2,1)S(1)} %get-tuple-element.114), channel_id=1, source_target_pairs={{0,1},{1,2},{2,3},{3,4},{4,5},{5,6},{6,7},{7,8},{8,9},{9,10},{10,1... | collective-permute-start | bytes 1179656 | tf_op jit(solution)/shard_map/ppermute | solution.py:15
  9.2 10.5 %collective-permute-start.1 = (bf16[2,384,256]{2,1,0:T(8,128)(2,1)S(1)}, bf16[2,384,256]{2,1,0:T(8,128)(2,1)S(1)}, u32[]{:S(2)}, u32[]{:S(2)}) collective-permute-start(bf16[2,384,256]{2,1,0:T(8,128)(2,1)S(1)} %get-tuple-element.115), channel_id=1, source_target_pairs={{1,0},{2,1},{3,2},{4,3},{5,4},{6,5},{7,6},{8,7},{9,8},{10,9},{11,1... | collective-permute-start | bytes 1179656 | tf_op jit(solution)/shard_map/ppermute | solution.py:18
  19.7 0.7 copy-start.3
  53.2 12.3 %copy-start.6 = (s32[2,64]{1,0:T(2,128)S(1)}, s32[2,64]{1,0:T(2,128)}, u32[]{:S(2)}) copy-start(s32[2,64]{1,0:T(2,128)} %param.16) | copy-start | bytes 1540
  70.9 57.3 %copy-start.4 = (f32[2,1024]{1,0:T(2,128)S(1)}, f32[2,1024]{1,0:T(2,128)}, u32[]{:S(2)}) copy-start(f32[2,1024]{1,0:T(2,128)} %param.23) | copy-start | bytes 24580
  72.4 55.8 %all-to-all-start = ((bf16[2,8,256,256]{3,2,0,1:T(8,128)(2,1)}), bf16[2,8,256,256]{3,2,0,1:T(8,128)(2,1)S(1)}, u32[]{:S(2)}, u32[]{:S(2)}) async-start(bf16[2,8,256,256]{3,2,0,1:T(8,128)(2,1)} %copy.38), calls=%async_computation | async-start | bytes 4194304 | tf_op jit(solution)/shard_map/all_to_all | solution.py:93
  128.2 2.2 copy-start.8
  131.8 2.2 copy-start.8
  135.4 2.2 copy-start.8
  139.0 2.2 copy-start.8
  142.6 2.2 copy-start.8
  146.1 2.2 copy-start.8
  149.7 2.2 copy-start.8
  153.3 2.2 copy-start.8
  156.9 2.2 copy-start.8
  160.5 2.2 copy-start.8
  164.1 2.2 copy-start.8
  167.6 2.2 copy-start.8
  171.2 2.2 copy-start.8
  174.8 2.2 copy-start.8
  178.4 2.2 copy-start.8
  182.0 2.2 copy-start.8
  185.6 55.1 %copy-start.5 = (bf16[256,256]{1,0:T(8,128)(2,1)S(1)}, bf16[256,256]{1,0:T(8,128)(2,1)}, u32[]{:S(2)}) copy-start(bf16[256,256]{1,0:T(8,128)(2,1)} %param.21) | copy-start | bytes 393220
  241.4 12.8 %copy-start.2 = (bf16[4096,256]{1,0:T(8,128)(2,1)}, bf16[4096,256]{1,0:T(8,128)(2,1)S(1)}, u32[]{:S(2)}) copy-start(bf16[4096,256]{1,0:T(8,128)(2,1)S(1)} %convolution_convert_fusion) | copy-start | bytes 6291460
  242.3 6.1 %collective-permute-start.2 = (bf16[2,384,256]{2,1,0:T(8,128)(2,1)S(1)}, bf16[2,384,256]{2,1,0:T(8,128)(2,1)S(1)}, u32[]{:S(2)}, u32[]{:S(2)}) collective-permute-start(bf16[2,384,256]{2,1,0:T(8,128)(2,1)S(1)} %get-tuple-element.112), channel_id=1, source_target_pairs={{0,1},{1,2},{2,3},{3,4},{4,5},{5,6},{6,7},{7,8},{8,9},{9,10},{10,1... | collective-permute-start | bytes 1179656 | tf_op jit(solution)/shard_map/ppermute | solution.py:15
  243.7 10.5 %collective-permute-start.3 = (bf16[2,384,256]{2,1,0:T(8,128)(2,1)S(1)}, bf16[2,384,256]{2,1,0:T(8,128)(2,1)S(1)}, u32[]{:S(2)}, u32[]{:S(2)}) collective-permute-start(bf16[2,384,256]{2,1,0:T(8,128)(2,1)S(1)} %get-tuple-element.113), channel_id=1, source_target_pairs={{1,0},{2,1},{3,2},{4,3},{5,4},{6,5},{7,6},{8,7},{9,8},{10,9},{11,1... | collective-permute-start | bytes 1179656 | tf_op jit(solution)/shard_map/ppermute | solution.py:18
  299.1 6.8 %copy-start.1 = (bf16[2,2048,256]{2,1,0:T(8,128)(2,1)S(1)}, bf16[2,2048,256]{2,1,0:T(8,128)(2,1)}, u32[]{:S(2)}) copy-start(bf16[2,2048,256]{2,1,0:T(8,128)(2,1)} %param.15) | copy-start | bytes 6291460
where the time goes:
time: 307 us; the launch traced here: 306 us
  local copies, waits for them, and re-layouts  73.4 us (24%)
  matrix products  72.1 us (23%)
  waiting for transfers between devices  70.3 us (23%)
  blocking collectives  54.9 us (18%)
  other arithmetic  24.2 us (8%)
  starting transfers between devices  10.1 us (3%)
    all_to_all x1, blocking collectives, shards(): lax.all_to_all(recurrent, 'snap', split_axis=0, concat_axis=1, tiled=True)  54.9 us
    all_to_all x1, waiting for transfers between devices, shards(): lax.all_to_all(grouped, 'snap', split_axis=1, concat_axis=0, tiled=True)  49.3 us
    gather x5, local copies, waits for them, and re-layouts, convolve(): jnp.take(slab, where_at, axis=0)  38.5 us
    dot_general x32, matrix products, cell_step(): jnp.dot(jnp.concatenate([inputs, hidden], axis=-1), weight, preferred_ele...  35.9 us
    dot_general x2, local copies, waits for them, and re-layouts, convolve(): jnp.einsum('skij,skjf->skif', tile_vals, picked, preferred_element_type=j...  24.5 us
    dot_general x2, matrix products, convolve(): jnp.einsum('skij,skjf->skif', tile_vals, picked, preferred_element_type=j...  23.2 us
    dynamic_update_slice x16, other arithmetic, shards(): lax.scan(advance, (zero_h, zero_c, zero_h, zero_c), sequence)  15.2 us
    ppermute x2, waiting for transfers between devices, with_halo(): lax.ppermute(lax.slice_in_dim(block, 0, width, axis=dim), axis, backward)  11.6 us
  transfers between devices with their start and end apart: 5, of which 5 were waited for; matrix products, arithmetic and copies ran while one was open for 0% of the time, Pallas kernels for 0%

commit v1 on v0

--- a/solution.py
+++ b/solution.py
@@ -103,9 +103,16 @@
 
     carry, outputs = lax.scan(advance, (zero_h, zero_c, zero_h, zero_c), sequence)
     recurrent = outputs[:, None]
-    restored = lax.all_to_all(recurrent, "snap", split_axis=0, concat_axis=1, tiled=True).reshape(
-        snapshots, vertices, width
+    begin_signs_now = lambda x_local, d_out, ndim_at: jnp.concatenate(
+        lax.all_to_all(
+            jnp.stack(jnp.split(x_local, lax.axis_size("snap"), axis=d_out)),
+            axis_name="snap",
+            split_axis=0,
+            concat_axis=0,
+        ),
+        axis=ndim_at,
     )
+    restored = begin_signs_now(recurrent, 0, 1).reshape(snapshots, vertices, width)
     second = project(restored, conv2_weight)
     return convolve(second, tile_rows, tile_cols, tile_vals, send_lists).astype(jnp.bfloat16)
 

time: 307 us -> 312 us (1.016)
  local copies, waits for them, and re-layouts: 73.4 us -> 78.6 us
    unnamed x16 -> x25, local copies, waits for them, and re-layouts: 1.33 us -> 6.63 us
where the time goes in v1:
time: 312 us; the launch traced here: 311 us
  local copies, waits for them, and re-layouts  78.6 us (25%)
  matrix products  72.4 us (23%)
  waiting for transfers between devices  70.3 us (23%)
  blocking collectives  53.7 us (17%)
  other arithmetic  24.2 us (8%)
  starting transfers between devices  10.3 us (3%)
    all_to_all x1, blocking collectives, shards(): lax.all_to_all(jnp.stack(jnp.split(x_local, lax.axis_size('snap'), axis=d...  53.7 us
    all_to_all x1, waiting for transfers between devices, shards(): lax.all_to_all(grouped, 'snap', split_axis=1, concat_axis=0, tiled=True)  49.3 us
    gather x5, local copies, waits for them, and re-layouts, convolve(): jnp.take(slab, where_at, axis=0)  38.5 us
    dot_general x32, matrix products, cell_step(): jnp.dot(jnp.concatenate([inputs, hidden], axis=-1), weight, preferred_ele...  36 us
    dot_general x2, local copies, waits for them, and re-layouts, convolve(): jnp.einsum('skij,skjf->skif', tile_vals, picked, preferred_element_type=j...  24.4 us
    dot_general x2, matrix products, convolve(): jnp.einsum('skij,skjf->skif', tile_vals, picked, preferred_element_type=j...  23.4 us
    dynamic_update_slice x16, other arithmetic, shards(): lax.scan(advance, (zero_h, zero_c, zero_h, zero_c), sequence)  15.2 us
    ppermute x2, waiting for transfers between devices, with_halo(): lax.ppermute(lax.slice_in_dim(block, 0, width, axis=dim), axis, backward)  11.6 us
  transfers between devices with their start and end apart: 5, of which 5 were waited for; matrix products, arithmetic and copies ran while one was open for 0% of the time, Pallas kernels for 0%

profile of v1, /device:TPU:31, one launch (start us, length us, event | category | flops | bytes accessed | tf_op | source)
XLA Modules:
  0.0 310.6 jit_solution(6708245566546643501)
XLA Ops:
  0.0 1.0 dynamic-slice_reduce_fusion
  1.6 2.9 convolution_convert_fusion.1
  4.5 2.2 gather_fusion
  7.0 2.2 collective-permute-start
  9.3 4.6 %collective-permute-done = bf16[2,384,256]{2,1,0:T(8,128)(2,1)S(1)} collective-permute-done((bf16[2,384,256]{2,1,0:T(8,128)(2,1)S(1)}, bf16[2,384,256]{2,1,0:T(8,128)(2,1)S(1)}, u32[]{:S(2)}, u32[]{:S(2)}) %collective-permute-start) | collective-permute-done | bytes 393248 | tf_op jit(solution)/shard_map/ppermute | solution.py:15
  13.9 5.8 %collective-permute-done.1 = bf16[2,384,256]{2,1,0:T(8,128)(2,1)S(1)} collective-permute-done((bf16[2,384,256]{2,1,0:T(8,128)(2,1)S(1)}, bf16[2,384,256]{2,1,0:T(8,128)(2,1)S(1)}, u32[]{:S(2)}, u32[]{:S(2)}) %collective-permute-start.1) | collective-permute-done | bytes 393248 | tf_op jit(solution)/shard_map/ppermute | solution.py:18
  20.5 1.9 pad_maximum_fusion
  22.4 7.2 %gather_fusion.1 = bf16[128,128,256]{2,1,0:T(8,128)(2,1)} fusion(bf16[2,22,128,256]{3,2,1,0:T(8,128)(2,1)S(1)} %bitcast.90, s32[128]{0:T(128)S(1)} %reshape.111), kind=kCustom, calls=%fused_computation.1.clone | custom fusion | bytes 16778240 | tf_op jit(solution)/shard_map/vmap(jit(_take))/gather | solution.py:47
  29.6 12.0 %copy.33 = bf16[2,64,128,256]{2,3,1,0:T(8,128)(2,1)} copy(bf16[2,64,128,256]{3,2,1,0:T(8,128)(2,1)} %bitcast.92) | data formatting | bytes 16777216 | tf_op jit(solution)/shard_map/vmap(jit(_take))/gather | solution.py:47
  41.6 11.7 %fusion.46 = bf16[2,64,128,256]{2,3,1,0:T(8,128)(2,1)} fusion(bf16[2,64,128,128]{3,2,1,0:T(8,128)(2,1)} %param.18, bf16[2,64,128,256]{2,3,1,0:T(8,128)(2,1)} %copy.33, pred[2,64]{1,0:T(4,128)(4,1)S(1)} %compare_and_fusion), kind=kOutput, calls=%fused_computation.64 | convolution fusion | flops 1077936128 | bytes 20971648 | tf_op jit(solution)/shard_map/skij,skjf->skif/dot_general | solution.py:48
  53.4 12.2 %copy.34 = bf16[2,64,128,256]{3,1,2,0:T(8,128)(2,1)} copy(bf16[2,64,128,256]{2,3,1,0:T(8,128)(2,1)} %fusion.46) | data formatting | bytes 16777216 | tf_op jit(solution)/shard_map/skij,skjf->skif/dot_general | solution.py:48
  65.6 4.6 %maximum_convert_fusion = bf16[2,16,128,256]{3,1,2,0:T(8,128)(2,1)S(1)} fusion(bf16[2,64,128,256]{3,1,2,0:T(8,128)(2,1)} %copy.34, s32[2,64]{1,0:T(2,128)S(1)} %copy-done.7), kind=kOutput, calls=%fused_computation.70 | convolution fusion | flops 137365504 | bytes 10486272 | tf_op jit(solution)/shard_map/skb,skif->sbif/dot_general | solution.py:50
  70.9 1.5 copy.36
  72.4 6.6 %all-to-all-start = ((bf16[2,8,256,256]{3,2,0,1:T(8,128)(2,1)}), bf16[2,8,256,256]{3,2,0,1:T(8,128)(2,1)S(1)}, u32[]{:S(2)}, u32[]{:S(2)}) async-start(bf16[2,8,256,256]{3,2,0,1:T(8,128)(2,1)} %copy.36), calls=%async_computation | async-start | bytes 4194304 | tf_op jit(solution)/shard_map/all_to_all | solution.py:93
  79.0 49.3 %all-to-all-done = bf16[2,8,256,256]{3,2,0,1:T(8,128)(2,1)S(1)} async-done(((bf16[2,8,256,256]{3,2,0,1:T(8,128)(2,1)}), bf16[2,8,256,256]{3,2,0,1:T(8,128)(2,1)S(1)}, u32[]{:S(2)}, u32[]{:S(2)}) %all-to-all-start) | async-done | bytes 2097184 | tf_op jit(solution)/shard_map/all_to_all | solution.py:93
  128.4 57.6 %while.19 = (s32[]{:T(128)}, bf16[256,256]{1,0:T(8,128)(2,1)S(1)}, f32[256,256]{1,0:T(8,128)S(1)}, bf16[256,256]{1,0:T(8,128)(2,1)S(1)}, f32[256,256]{1,0:T(8,12...) while((s32[]{:T(128)}, bf16[256,256]{1,0:T(8,128)(2,1)S(1)}, ...), condition=%wide.region_1.4_spmd.clone, body=%wide.region_0.0_spmd.clone.sunk | while | flops 540540928 | bytes 17457816 | solution.py:104
  128.5 1.8 convolution_add_fusion.4
  131.0 0.9 bitcast_dynamic-update-slice_fusion.10
  132.1 1.8 convolution_add_fusion.4
  135.7 1.8 convolution_add_fusion.4
  139.3 1.8 convolution_add_fusion.4
  142.9 1.8 convolution_add_fusion.4
  146.5 1.8 convolution_add_fusion.4
  150.1 1.8 convolution_add_fusion.4
  153.7 1.8 convolution_add_fusion.4
  157.3 1.8 convolution_add_fusion.4
  160.9 1.8 convolution_add_fusion.4
  164.5 1.8 convolution_add_fusion.4
  168.1 1.8 convolution_add_fusion.4
  171.7 1.8 convolution_add_fusion.4
  175.3 1.8 convolution_add_fusion.4
  178.9 1.8 convolution_add_fusion.4
  182.5 1.8 convolution_add_fusion.4
  186.0 1.1 bitcast_dynamic-update-slice_fusion.8
  187.1 1.0 bitcast_dynamic-update-slice_fusion.7
  188.1 1.0 bitcast_dynamic-update-slice_fusion.6
  189.1 1.0 bitcast_dynamic-update-slice_fusion.5
  190.2 53.7 %all_to_all.20 = bf16[8,2,1,256,256]{4,3,1,2,0:T(8,128)(2,1)S(1)} all-to-all(bf16[8,2,1,256,256]{4,3,1,2,0:T(8,128)(2,1)S(1)} %bitcast_dynamic-update-slice_fusion.1), channel_id=1, replica_groups=mesh['snap'=8,'vert'=32] {'snap'}, dimensions={0} | all-to-all | bytes 4194304 | tf_op jit(solution)/shard_map/all_to_all | solution.py:107
  246.9 1.4 collective-permute-start.2
  248.3 4.7 %collective-permute-done.2 = bf16[2,384,256]{2,1,0:T(8,128)(2,1)S(1)} collective-permute-done((bf16[2,384,256]{2,1,0:T(8,128)(2,1)S(1)}, bf16[2,384,256]{2,1,0:T(8,128)(2,1)S(1)}, u32[]{:S(2)}, u32[]{:S(2)}) %collective-permute-start.2) | collective-permute-done | bytes 393248 | tf_op jit(solution)/shard_map/ppermute | solution.py:15
  253.0 5.8 %collective-permute-done.3 = bf16[2,384,256]{2,1,0:T(8,128)(2,1)S(1)} collective-permute-done((bf16[2,384,256]{2,1,0:T(8,128)(2,1)S(1)}, bf16[2,384,256]{2,1,0:T(8,128)(2,1)S(1)}, u32[]{:S(2)}, u32[]{:S(2)}) %collective-permute-start.3) | collective-permute-done | bytes 393248 | tf_op jit(solution)/shard_map/ppermute | solution.py:18
  258.8 1.8 pad_maximum_fusion.1
  260.6 7.2 %gather_fusion.3 = bf16[128,128,256]{2,1,0:T(8,128)(2,1)} fusion(bf16[2,22,128,256]{3,2,1,0:T(8,128)(2,1)S(1)} %bitcast.89, s32[128]{0:T(128)S(1)} %reshape.111), kind=kCustom, calls=%fused_computation.3.clone | custom fusion | bytes 16778240 | tf_op jit(solution)/shard_map/vmap(jit(_take))/gather | solution.py:47
  267.8 12.0 %copy.39 = bf16[2,64,128,256]{2,3,1,0:T(8,128)(2,1)} copy(bf16[2,64,128,256]{3,2,1,0:T(8,128)(2,1)} %bitcast.91) | data formatting | bytes 16777216 | tf_op jit(solution)/shard_map/vmap(jit(_take))/gather | solution.py:47
  279.8 11.7 %fusion.49 = bf16[2,64,128,256]{2,3,1,0:T(8,128)(2,1)} fusion(bf16[2,64,128,128]{3,2,1,0:T(8,128)(2,1)} %param.18, bf16[2,64,128,256]{2,3,1,0:T(8,128)(2,1)} %copy.39, pred[2,64]{1,0:T(4,128)(4,1)S(1)} %compare_and_fusion), kind=kOutput, calls=%fused_computation.65 | convolution fusion | flops 1077936128 | bytes 20971648 | tf_op jit(solution)/shard_map/skij,skjf->skif/dot_general | solution.py:48
  291.6 12.2 %copy.40 = bf16[2,64,128,256]{3,1,2,0:T(8,128)(2,1)} copy(bf16[2,64,128,256]{2,3,1,0:T(8,128)(2,1)} %fusion.49) | data formatting | bytes 16777216 | tf_op jit(solution)/shard_map/skij,skjf->skif/dot_general | solution.py:48
  303.8 4.7 %convolution_convert_fusion.2 = bf16[2,16,128,256]{3,1,2,0:T(8,128)(2,1)S(1)} fusion(bf16[2,64,128,256]{3,1,2,0:T(8,128)(2,1)} %copy.40, s32[2,64]{1,0:T(2,128)S(1)} %copy-done.7), kind=kOutput, calls=%fused_computation.73 | convolution fusion | flops 134219776 | bytes 10486272 | tf_op jit(solution)/shard_map/skb,skif->sbif/dot_general | solution.py:50
  308.5 2.1 copy.41
  (172 shorter events, 32.3 us)
Async XLA Ops:
  0.0 1.6 copy-start
  6.7 2.5 copy-start.8
  7.0 6.9 %collective-permute-start = (bf16[2,384,256]{2,1,0:T(8,128)(2,1)S(1)}, bf16[2,384,256]{2,1,0:T(8,128)(2,1)S(1)}, u32[]{:S(2)}, u32[]{:S(2)}) collective-permute-start(bf16[2,384,256]{2,1,0:T(8,128)(2,1)S(1)} %get-tuple-element.114), channel_id=1, source_target_pairs={{0,1},{1,2},{2,3},{3,4},{4,5},{5,6},{6,7},{7,8},{8,9},{9,10},{10,1... | collective-permute-start | bytes 1179656 | tf_op jit(solution)/shard_map/ppermute | solution.py:15
  9.2 10.5 %collective-permute-start.1 = (bf16[2,384,256]{2,1,0:T(8,128)(2,1)S(1)}, bf16[2,384,256]{2,1,0:T(8,128)(2,1)S(1)}, u32[]{:S(2)}, u32[]{:S(2)}) collective-permute-start(bf16[2,384,256]{2,1,0:T(8,128)(2,1)S(1)} %get-tuple-element.115), channel_id=1, source_target_pairs={{1,0},{2,1},{3,2},{4,3},{5,4},{6,5},{7,6},{8,7},{9,8},{10,9},{11,1... | collective-permute-start | bytes 1179656 | tf_op jit(solution)/shard_map/ppermute | solution.py:18
  19.7 0.8 copy-start.4
  53.3 12.2 %copy-start.7 = (s32[2,64]{1,0:T(2,128)S(1)}, s32[2,64]{1,0:T(2,128)}, u32[]{:S(2)}) copy-start(s32[2,64]{1,0:T(2,128)} %param.16) | copy-start | bytes 1540
  72.4 56.0 %copy-start.5 = (f32[2,1024]{1,0:T(2,128)S(1)}, f32[2,1024]{1,0:T(2,128)}, u32[]{:S(2)}) copy-start(f32[2,1024]{1,0:T(2,128)} %param.23) | copy-start | bytes 24580
  72.4 56.0 %all-to-all-start = ((bf16[2,8,256,256]{3,2,0,1:T(8,128)(2,1)}), bf16[2,8,256,256]{3,2,0,1:T(8,128)(2,1)S(1)}, u32[]{:S(2)}, u32[]{:S(2)}) async-start(bf16[2,8,256,256]{3,2,0,1:T(8,128)(2,1)} %copy.36), calls=%async_computation | async-start | bytes 4194304 | tf_op jit(solution)/shard_map/all_to_all | solution.py:93
  128.4 2.1 copy-start.9
  132.0 2.1 copy-start.9
  135.6 2.1 copy-start.9
  139.2 2.1 copy-start.9
  142.8 2.1 copy-start.9
  146.4 2.1 copy-start.9
  150.0 2.1 copy-start.9
  153.6 2.1 copy-start.9
  157.2 2.1 copy-start.9
  160.8 2.1 copy-start.9
  164.4 2.1 copy-start.9
  168.0 2.1 copy-start.9
  171.6 2.1 copy-start.9
  175.2 2.1 copy-start.9
  178.8 2.1 copy-start.9
  182.4 2.1 copy-start.9
  186.0 4.0 %copy-start.3 = (bf16[16,256,256]{2,1,0:T(8,128)(2,1)S(1)}, bf16[16,256,256]{2,1,0:T(8,128)(2,1)}, u32[]{:S(2)}) copy-start(bf16[16,256,256]{2,1,0:T(8,128)(2,1)} %get-tuple-element.54) | copy-start | bytes 6291460
  243.9 0.9 copy-start.6
  245.5 1.3 copy-start.2
  246.9 6.2 %collective-permute-start.2 = (bf16[2,384,256]{2,1,0:T(8,128)(2,1)S(1)}, bf16[2,384,256]{2,1,0:T(8,128)(2,1)S(1)}, u32[]{:S(2)}, u32[]{:S(2)}) collective-permute-start(bf16[2,384,256]{2,1,0:T(8,128)(2,1)S(1)} %get-tuple-element.112), channel_id=1, source_target_pairs={{0,1},{1,2},{2,3},{3,4},{4,5},{5,6},{6,7},{7,8},{8,9},{9,10},{10,1... | collective-permute-start | bytes 1179656 | tf_op jit(solution)/shard_map/ppermute | solution.py:15
  248.3 10.5 %collective-permute-start.3 = (bf16[2,384,256]{2,1,0:T(8,128)(2,1)S(1)}, bf16[2,384,256]{2,1,0:T(8,128)(2,1)S(1)}, u32[]{:S(2)}, u32[]{:S(2)}) collective-permute-start(bf16[2,384,256]{2,1,0:T(8,128)(2,1)S(1)} %get-tuple-element.113), channel_id=1, source_target_pairs={{1,0},{2,1},{3,2},{4,3},{5,4},{6,5},{7,6},{8,7},{9,8},{10,9},{11,1... | collective-permute-start | bytes 1179656 | tf_op jit(solution)/shard_map/ppermute | solution.py:18
  303.8 6.8 %copy-start.1 = (bf16[2,2048,256]{2,1,0:T(8,128)(2,1)S(1)}, bf16[2,2048,256]{2,1,0:T(8,128)(2,1)}, u32[]{:S(2)}) copy-start(bf16[2,2048,256]{2,1,0:T(8,128)(2,1)} %param.15) | copy-start | bytes 6291460
